TPU v7x, 256 devices: a whole 4x4x8 slice. The times are simulated.
256 devices in a mesh: seq: 128 (over z, x, y), head: 2 (over core).
Axes of the slice: x: 4, y: 4, z: 8, core: 2. Of those that a mesh axis runs over, the one named last changes fastest.
Arguments:
- queries: bfloat16 [32768, 32, 128], P('seq', 'head'), may hold values from -192 to 192
- keys: bfloat16 [32768, 8, 128], P(('seq', 'head')), may hold values from -6 to 6
- values: bfloat16 [32768, 8, 128], P(('seq', 'head')), may hold values from -6 to 6
- doc_start: int32 [32768], P('seq'), may hold values from 0 to 32767, as said below
- tile_list: int32 [128, 18], P('seq'), may hold values from 0 to 255, as said below
- tile_count: int32 [128], P('seq'), may hold values from 2 to 18, as said below
Outputs:
- attention_out: bfloat16 [32768, 32, 128], P('seq', 'head')
Inputs may be any that keep to these rules, and one draw needn't show every extreme that they name: doc_start never falls, doc_start[i] <= i, and a new document begins at each position where it changes; documents hold 1 to 2048 tokens, one exactly 2048. `tile_list`: row s holds in its first tile_count[s] entries, ascending, exactly the tiles (tile t holds key positions t * 128 to t * 128 + 127) that contain a key visible to some query of positions s * 256 to s * 256 + 255; the later entries equal s * 2. `tile_count`: some row reaches 18.
All inputs are finite; a program needn't handle non-finite values.
Results may differ from a plain program's by a relative error of at most 0.004.
Values may be sent and summed in bfloat16 or wider, within the bound.
A program may use at most 64 MiB of HBM per device.

v0:
```python
import jax
import jax.numpy as jnp
from jax import lax
from jax.experimental import pallas as pl
from jax.experimental.pallas import tpu as pltpu
from jax.sharding import PartitionSpec as P

TILE = 128
REACH = 8
BACK = REACH + 1
SIDE = 4
HEADS = 4
GROUP = 4
TOK = 256
HD = 128
ENTRIES = BACK * HEADS
FIRST = 2
NEG = -1e30
FAR = 1 << 20
MESH = pl.DeviceIdType.MESH

PLAN = (
    (54547458, 326392868, 309400822, 553747682, 503431366, 274251856, 339108337, 151355832, 184951328, 495388016, 537034880, 218448288),
    (5279796, 309644368, 271925456, 394514453, 205652514, 289884273, 169332072, 471957680, 155732196, 505987401, 67502496, 537313680),
    (4247573, 37815575, 134603059, 276144324, 556163184, 253855040, 151082279, 189202642, 587637248, 570655202, 352831649, 453460352),
    (54562820, 207699988, 497325315, 134536528, 394780880, 471096760, 505659720, 436767856, 590512304, 378601856, 537022995, 235290720),
)


def attend(queries_t, window, thresholds, top, total, summed, back, head, own):
    scale = HD ** (-0.5) * 1.4426950408889634
    key_tile = window[back, head, 0]
    value_tile = window[back, head, 1]
    iota = lax.broadcasted_iota(jnp.int32, (TILE, TOK), 0)
    for member in range(GROUP):
        span = slice(member * TOK, (member + 1) * TOK)
        scores = jnp.dot(
            key_tile, queries_t[head, :, span], preferred_element_type=jnp.float32
        )
        halves = []
        for half in range(2):
            low = thresholds[pl.ds(back * 2 + half, 1), :]
            seen = iota >= low
            if own:
                seen = seen & (
                    iota + half * TILE <= lax.broadcasted_iota(jnp.int32, (TILE, TOK), 1)
                )
            halves.append(jnp.where(seen, scores[half * TILE : (half + 1) * TILE], NEG))
        scores = jnp.concatenate(halves, axis=0)
        new_top = jnp.max(scores, axis=0, keepdims=True)
        if not own:
            old_top = top[head, :, span]
            new_top = jnp.maximum(old_top, new_top)
        scaled_top = new_top * scale
        weights = jnp.exp2(scores * scale - scaled_top)
        weight_sum = jnp.sum(weights, axis=0, keepdims=True)
        product = lax.dot_general(
            value_tile,
            weights.astype(jnp.bfloat16),
            (((0,), (0,)), ((), ())),
            preferred_element_type=jnp.float32,
        )
        if not own:
            factor = jnp.exp2(old_top * scale - scaled_top)
            weight_sum = total[head, :, span] * factor + weight_sum
            product = summed[head, :, span] * factor + product
        top[head, :, span] = new_top
        total[head, :, span] = weight_sum
        summed[head, :, span] = product


def kernel(
    q_ref,
    k_ref,
    v_ref,
    start_ref,
    list_ref,
    count_ref,
    o_ref,
    window,
    queries_t,
    thresholds,
    top,
    total,
    summed,
    result,
    local_sem,
    swap_send,
    swap_recv,
    send_sem,
    recv_sem,
):
    seq = lax.axis_index("seq")
    core = lax.axis_index("head")
    devices = lax.axis_size("seq")
    place = lax.rem(seq, SIDE)
    row_first = seq - place
    neighbours = (
        row_first + lax.rem(place + 1, SIDE),
        row_first + lax.rem(place + SIDE - 1, SIDE),
        lax.rem(seq + SIDE, devices),
        lax.rem(seq + devices - SIDE, devices),
    )
    last = place == SIDE - 1
    none = place == 0
    shifts = (
        jnp.where(last, 1 - SIDE, 1),
        jnp.where(none, SIDE - 1, -1),
        SIDE,
        -SIDE,
    )

    barrier = pltpu.get_barrier_semaphore()
    for where in neighbours:
        pl.semaphore_signal(
            barrier, inc=1, device_id=(where, core), device_id_type=MESH
        )
    pl.semaphore_signal(barrier, inc=1, device_id=(seq, 1 - core), device_id_type=MESH)

    locals_ = []
    for part, ref in enumerate((k_ref, v_ref)):
        locals_.append(
            pltpu.make_async_copy(
                ref.at[pl.ds(core * HEADS, HEADS)],
                window.at[0, :, part, pl.ds(core * TILE, TILE), :],
                local_sem.at[part],
            )
        )
    for copy in locals_:
        copy.start()
    pl.semaphore_wait(barrier, 5)
    swaps = []
    for part, ref in enumerate((k_ref, v_ref)):
        swaps.append(
            pltpu.make_async_remote_copy(
                src_ref=ref.at[pl.ds((1 - core) * HEADS, HEADS)],
                dst_ref=window.at[0, :, part, pl.ds(core * TILE, TILE), :],
                send_sem=swap_send.at[part],
                recv_sem=swap_recv.at[part],
                device_id=(seq, 1 - core),
                device_id_type=MESH,
            )
        )
    for copy in swaps:
        copy.start()

    tile_row = lax.broadcasted_iota(jnp.int32, (24, 1), 0)
    back_of = tile_row // 2
    half_of = tile_row - 2 * back_of
    tile_id = 2 * (seq - back_of) + half_of
    slots = list_ref.shape[1]
    listed = (list_ref[...] == tile_id) & (
        lax.broadcasted_iota(jnp.int32, (1, slots), 1) < count_ref[0]
    )
    live = jnp.max(jnp.where(listed, 1.0, 0.0), axis=1, keepdims=True)
    low = start_ref[...] - seq * TOK + (back_of * TOK - half_of * TILE)
    thresholds[...] = jnp.where(live > 0.5, low, FAR)

    for head in range(HEADS):
        for member in range(GROUP):
            queries_t[head, :, member * TOK : (member + 1) * TOK] = q_ref[
                :, head * GROUP + member, :
            ].T

    def hand_on(slot, part, direction):
        back, head = slot // HEADS, lax.rem(slot, HEADS)
        there = back + shifts[direction]
        return pltpu.make_async_remote_copy(
            src_ref=window.at[back, head, part],
            dst_ref=window.at[there, head, part],
            send_sem=send_sem.at[slot, part, direction],
            recv_sem=recv_sem.at[there * HEADS + head, part],
            device_id=(neighbours[direction], core),
            device_id_type=MESH,
        )

    def arrived(slot, part):
        back, head = slot // HEADS, lax.rem(slot, HEADS)
        return pltpu.make_async_remote_copy(
            src_ref=window.at[back, head, part],
            dst_ref=window.at[back, head, part],
            send_sem=send_sem.at[slot, part, 0],
            recv_sem=recv_sem.at[slot, part],
            device_id=(neighbours[0], core),
            device_id_type=MESH,
        )

    words = []
    for j in range(ENTRIES // 3):
        word = PLAN[0][j]
        for c in range(1, SIDE):
            word = jnp.where(place == c, PLAN[c][j], word)
        words.append(word)

    def entry(n):
        j, third = n // 3, lax.rem(n, 3)
        word = words[0]
        for i in range(1, ENTRIES // 3):
            word = jnp.where(j == i, words[i], word)
        divisor = jnp.where(third == 0, 1, jnp.where(third == 1, 1024, 1048576))
        code = lax.rem(word // divisor, 1024)
        return code // 16, lax.rem(code, 16)

    def relay(slot, directions):
        for part in range(2):

            @pl.when(slot >= HEADS)
            def _():
                arrived(slot, part).wait_recv()

            for direction in range(4):

                @pl.when(lax.rem(directions // (1 << direction), 2) == 1)
                def _():
                    hand_on(slot, part, direction).start()

    for copy in locals_:
        copy.wait()
    for copy in swaps:
        copy.wait()

    for n in range(FIRST):
        relay(*entry(n))
    for head in range(HEADS):
        attend(queries_t, window, thresholds, top, total, summed, 0, head, True)

    def step(n, _):
        slot, directions = entry(n)
        relay(slot, directions)

        @pl.when(slot >= HEADS)
        def _():
            back, head = slot // HEADS, lax.rem(slot, HEADS)
            attend(queries_t, window, thresholds, top, total, summed, back, head, False)

        return 0

    lax.fori_loop(FIRST, ENTRIES, step, 0)

    for head in range(HEADS):
        for member in range(GROUP):
            span = slice(member * TOK, (member + 1) * TOK)
            inverse = 1.0 / total[head, :, span]
            result[:, head * GROUP + member, :] = (summed[head, :, span] * inverse).T
    o_ref[...] = result[...].astype(jnp.bfloat16)

    def finish(n, _):
        slot, directions = entry(n)
        for part in range(2):
            for direction in range(4):

                @pl.when(lax.rem(directions // (1 << direction), 2) == 1)
                def _():
                    hand_on(slot, part, direction).wait_send()

        return 0

    lax.fori_loop(0, ENTRIES, finish, 0)


def body(queries, keys, values, doc_start, tile_list, tile_count):
    keys_t = jnp.swapaxes(keys, 0, 1)
    values_t = jnp.swapaxes(values, 0, 1)
    vmem = pl.BlockSpec(memory_space=pltpu.VMEM)
    hbm = pl.BlockSpec(memory_space=pltpu.HBM)
    lanes = GROUP * TOK
    return pl.pallas_call(
        kernel,
        out_shape=jax.ShapeDtypeStruct(queries.shape, jnp.bfloat16),
        in_specs=[vmem, hbm, hbm, vmem, vmem, pl.BlockSpec(memory_space=pltpu.SMEM)],
        out_specs=vmem,
        scratch_shapes=[
            pltpu.VMEM((BACK, HEADS, 2, TOK, HD), jnp.bfloat16),
            pltpu.VMEM((HEADS, HD, lanes), jnp.bfloat16),
            pltpu.VMEM((24, TOK), jnp.int32),
            pltpu.VMEM((HEADS, 1, lanes), jnp.float32),
            pltpu.VMEM((HEADS, 1, lanes), jnp.float32),
            pltpu.VMEM((HEADS, HD, lanes), jnp.float32),
            pltpu.VMEM(queries.shape, jnp.float32),
            pltpu.SemaphoreType.DMA((2,)),
            pltpu.SemaphoreType.DMA((2,)),
            pltpu.SemaphoreType.DMA((2,)),
            pltpu.SemaphoreType.DMA((ENTRIES, 2, 4)),
            pltpu.SemaphoreType.DMA((ENTRIES, 2)),
        ],
        compiler_params=pltpu.CompilerParams(collective_id=0, has_side_effects=True),
    )(queries, keys_t, values_t, doc_start.reshape(1, TOK), tile_list, tile_count)


def solution(mesh):
    in_specs = (
        P("seq", "head", None),
        P(("seq", "head"), None, None),
        P(("seq", "head"), None, None),
        P("seq"),
        P("seq", None),
        P("seq"),
    )
    return jax.shard_map(
        body, mesh=mesh, in_specs=in_specs, out_specs=P("seq", "head", None), check_vma=False
    )
```

profile of v0, /device:TPU:1, one launch (start us, length us, event | category | flops | bytes accessed | tf_op | source)
XLA Modules:
  0.0 82.4 jit_solution(3015534377364566518)
XLA Ops:
  0.7 1.9 %copy_bitcast_fusion = (bf16[8,128,128]{2,1,0:T(8,128)(2,1)}, bf16[8,128,128]{2,1,0:T(8,128)(2,1)}) fusion(bf16[128,8,128]{2,1,0:T(8,128)(2,1)} %param.8, bf16[128,8,128]{2,1,0:T(8,128)(2,1)} %param.7), kind=kLoop, calls=%fused_computation | loop fusion | bytes 1048576 | tf_op jit(solution)/shard_map/transpose | solution.py:263
  2.6 77.4 %shard_map.64 = bf16[256,16,128]{2,1,0:T(8,128)(2,1)} custom-call(bf16[256,16,128]{2,1,0:T(8,128)(2,1)} %q_ref.1, bf16[8,128,128]{2,1,0:T(8,128)(2,1)} %get-tuple-element.6.k_ref, bf16[8,128,128]{2,1,0:T(8,128)(2,1)} %get-tuple-element.5.v_ref, s32[1,256]{1,0:T(1,128)} %bitcast.5, s32[1,18]{1,0:T(1,128)} %list_ref.1, s32[1]{0:T(128)S(6)} %copy.12.count_ref), custom_call_target="tpu_custom_call" | custom-call | tf_op jit(solution)/shard_map/pallas_call | solution.py:267
  80.0 2.4 %copy.13 = bf16[256,16,128]{2,1,0:T(8,128)(2,1)} copy(bf16[256,16,128]{2,1,0:T(8,128)(2,1)} %shard_map.64) | data formatting | bytes 2097152
where the time goes:
time: 82.5 us; the launch traced here: 82.4 us
  Pallas kernels  77.4 us (94%)
  local copies, waits for them, and re-layouts  4.29 us (5%)
    pallas_call x1, Pallas kernels, body(): pl.pallas_call(kernel, out_shape=jax.ShapeDtypeStruct(queries.shape, jnp....  77.4 us
    unnamed x1, local copies, waits for them, and re-layouts  2.37 us
    transpose x1, local copies, waits for them, and re-layouts, body(): values_t = jnp.swapaxes(values, 0, 1)  1.92 us

commit v1 on v0

--- a/solution.py
+++ b/solution.py
@@ -15,15 +15,36 @@
 HD = 128
 ENTRIES = BACK * HEADS
 FIRST = 2
+TURN = 5
 NEG = -1e30
 FAR = 1 << 20
 MESH = pl.DeviceIdType.MESH
 
 PLAN = (
-    (54547458, 326392868, 309400822, 553747682, 503431366, 274251856, 339108337, 151355832, 184951328, 495388016, 537034880, 218448288),
-    (5279796, 309644368, 271925456, 394514453, 205652514, 289884273, 169332072, 471957680, 155732196, 505987401, 67502496, 537313680),
-    (4247573, 37815575, 134603059, 276144324, 556163184, 253855040, 151082279, 189202642, 587637248, 570655202, 352831649, 453460352),
-    (54562820, 207699988, 497325315, 134536528, 394780880, 471096760, 505659720, 436767856, 590512304, 378601856, 537022995, 235290720),
+    (133376, 134400, 137664, 138688, 131264, 132288, 166336, 167377, 135360, 136384, 170368, 162048, 143680, 171411, 163087, 144704, 198662, 157952, 145472, 199713, 158989, 202752, 146503, 160128, 194624, 139264, 151680, 176256, 140292, 161152, 203790, 141411, 152704, 195658, 142431, 177280, 180741, 178176, 190528, 181782, 179224, 147456, 191552, 149527, 153885, 192576, 188928, 172032, 193600, 148480, 189982, 164168, 150556, 186368, 154889, 155648, 168203, 173076, 184320, 156672, 196608, 165196, 182288, 187392, 174107, 169234, 175104, 200725, 183321, 197632, 185376, 26, 201762, 0, 0, 0, 0, 0, 0, 0),
+    (137536, 138560, 133440, 134464, 135424, 136448, 170112, 131392, 132416, 171155, 145408, 166080, 146439, 155904, 167121, 139328, 156940, 168128, 140356, 159872, 169170, 174592, 160910, 164096, 175637, 161792, 165136, 143616, 162831, 141376, 188608, 144646, 142400, 189632, 158080, 151557, 28, 196736, 147712, 152586, 197760, 159136, 153869, 176320, 192640, 154891, 190592, 148744, 202752, 177344, 184342, 149824, 191616, 193693, 203806, 180224, 185344, 150883, 26, 186432, 194560, 198665, 181248, 178200, 199713, 187456, 195584, 200731, 31, 182272, 179200, 201751, 34, 183296, 172057, 173076, 0, 0, 0, 0),
+    (131392, 132416, 135488, 136512, 137472, 138496, 145472, 164032, 146503, 133440, 134464, 165072, 141312, 168320, 142341, 160000, 169362, 139584, 161038, 170432, 140612, 161792, 171475, 174144, 162831, 166336, 175189, 155776, 167377, 147456, 200832, 176128, 156812, 192640, 148488, 182272, 201890, 177152, 183318, 193689, 149504, 151582, 202880, 196608, 152586, 172032, 150537, 187008, 203939, 197632, 188448, 173076, 184320, 188059, 198656, 180224, 153600, 185370, 199680, 178209, 157952, 154635, 189468, 158976, 181261, 24, 194560, 143360, 190464, 179223, 195615, 144390, 191517, 0, 0, 0, 0, 0, 0, 0),
+    (135424, 136448, 137472, 138496, 139264, 168128, 140292, 131328, 132352, 133376, 134400, 169170, 143360, 161792, 170432, 144390, 162831, 171456, 153875, 155904, 172032, 164288, 156940, 154891, 165312, 191120, 141312, 166208, 192157, 142341, 167232, 160145, 173056, 157696, 202836, 161166, 147712, 203840, 158720, 194723, 178765, 196800, 195743, 148736, 188616, 184832, 145408, 179799, 186496, 176128, 182784, 197856, 200704, 146439, 174080, 189632, 185884, 151680, 183834, 198720, 177177, 175104, 187542, 201749, 149504, 199771, 34, 152704, 192545, 150538, 193545, 180254, 181272, 0, 0, 0, 0, 0, 0, 0),
+    (133376, 134400, 137664, 138688, 131264, 132288, 166336, 167377, 135360, 136384, 170368, 162048, 143680, 171411, 163087, 144704, 198662, 157952, 199713, 145472, 158989, 202752, 146503, 160128, 194624, 139264, 151680, 176256, 140292, 161152, 203790, 141411, 152704, 195658, 142400, 180767, 177285, 178176, 149504, 190550, 179223, 181760, 191576, 153856, 147456, 150528, 192605, 164169, 188928, 193630, 154891, 189952, 148508, 172032, 184328, 186368, 165200, 155648, 168192, 173076, 156672, 169216, 196620, 174098, 182272, 187419, 175104, 185365, 200730, 183321, 197664, 201762, 0, 0, 0, 0, 0, 0, 0, 0),
+    (137536, 138560, 133440, 134464, 170112, 135424, 136448, 171155, 131392, 132416, 145408, 166080, 155904, 146432, 167111, 156945, 139328, 168140, 159872, 140352, 169156, 18, 160896, 174592, 164110, 161792, 175616, 165141, 16, 162816, 143616, 188623, 158080, 141376, 144640, 189638, 28, 159104, 142400, 151552, 196749, 147717, 152576, 197770, 192640, 153856, 176352, 148744, 154880, 177355, 184342, 202752, 190592, 193694, 149824, 180224, 185370, 203776, 191651, 194589, 150848, 186441, 178176, 198656, 187483, 195615, 199680, 181281, 179224, 200704, 182295, 172032, 183321, 201762, 173076, 0, 0, 0, 0, 0),
+    (131392, 132416, 135488, 136512, 137472, 138496, 164032, 145472, 165056, 146512, 133440, 134471, 168320, 141312, 160000, 169362, 142341, 161024, 170446, 139584, 171456, 161811, 140612, 166336, 162816, 174159, 167377, 175168, 155797, 200832, 147456, 156812, 192640, 176128, 182272, 201890, 148480, 183304, 172057, 177152, 151574, 193664, 196638, 152586, 202880, 149504, 178176, 173076, 197632, 187040, 203939, 150528, 180233, 198656, 184320, 188059, 199713, 185344, 153600, 188442, 157952, 181272, 154635, 179223, 158989, 189468, 194560, 143360, 190464, 195615, 144390, 191517, 0, 0, 0, 0, 0, 0, 0, 0),
+    (135424, 136448, 137472, 138496, 139264, 168128, 140288, 169156, 131328, 132352, 133376, 134418, 143360, 170432, 161792, 144390, 171456, 162835, 172047, 164288, 155904, 153856, 165328, 156940, 173056, 166208, 191124, 154891, 167232, 192145, 141341, 202816, 160128, 142341, 157696, 203840, 161187, 178752, 186496, 158720, 194702, 13, 147712, 188608, 195743, 179799, 196800, 184832, 145408, 148744, 189632, 176156, 174080, 187547, 200704, 146439, 182784, 197824, 185888, 151680, 175130, 198720, 177173, 183808, 199766, 201728, 149529, 192545, 152738, 193546, 150558, 180233, 181272, 0, 0, 0, 0, 0, 0, 0),
+    (133376, 134400, 137664, 138688, 131264, 132288, 166336, 167377, 135360, 136384, 170368, 162048, 143680, 171411, 163087, 144704, 198662, 157952, 199713, 145472, 158989, 202752, 146503, 160128, 194624, 139264, 151680, 176256, 140292, 161152, 203790, 141411, 152704, 195658, 142400, 180767, 177285, 178176, 149504, 190550, 179223, 181760, 191576, 147456, 153856, 150528, 192605, 9, 172032, 188928, 193630, 164160, 189952, 148508, 8, 186368, 154880, 184331, 196608, 173056, 155668, 168192, 187419, 165184, 156672, 182288, 174092, 169216, 197650, 175104, 185376, 200725, 183322, 201753, 34, 0, 0, 0, 0, 0),
+    (137536, 138560, 133440, 134464, 170112, 135424, 136448, 171155, 131392, 132416, 145408, 166080, 155904, 146432, 167111, 156945, 139328, 168140, 159872, 140352, 169156, 18, 160896, 174592, 164110, 161792, 175616, 165141, 16, 162816, 143616, 188623, 158080, 141376, 144640, 189638, 28, 159104, 142400, 151552, 196749, 147717, 152576, 197770, 192640, 153856, 176352, 148744, 154880, 190603, 184320, 202752, 177366, 193694, 149824, 191645, 185370, 203776, 180259, 194560, 150848, 186441, 195615, 198656, 181272, 178176, 199680, 187489, 27, 179200, 200704, 182295, 201728, 183330, 25, 172032, 173076, 0, 0, 0),
+    (131392, 132416, 135488, 136512, 137472, 138496, 164032, 145472, 165056, 146512, 133440, 134471, 168320, 141312, 160000, 169362, 142341, 161024, 170446, 139584, 171456, 161811, 140612, 166336, 162816, 174159, 167377, 175168, 155797, 200832, 147456, 156812, 192640, 176128, 182272, 201890, 148480, 183304, 193689, 177152, 151582, 202880, 196630, 152586, 172032, 149504, 188416, 203939, 197632, 187040, 173076, 150528, 180233, 198656, 184320, 188059, 199713, 185344, 153600, 178202, 157952, 189468, 154635, 181272, 158989, 143360, 190464, 194560, 179223, 195615, 144390, 191517, 0, 0, 0, 0, 0, 0, 0, 0),
+    (135424, 136448, 137472, 138496, 139264, 168128, 140288, 169156, 131328, 132352, 133376, 134418, 143360, 170432, 161792, 144390, 171456, 162835, 172047, 164288, 155904, 153856, 165328, 156940, 173056, 166208, 191124, 154891, 167232, 192145, 141341, 202816, 160128, 142341, 157696, 203840, 161187, 178766, 196800, 158720, 194701, 147712, 188608, 195743, 179799, 186496, 184832, 145408, 148744, 197824, 176160, 174080, 189660, 200704, 146432, 182791, 198720, 185882, 151680, 175104, 187541, 177179, 183808, 199744, 201750, 149529, 192545, 152738, 193546, 150528, 180254, 9, 181272, 0, 0, 0, 0, 0, 0, 0),
+    (133376, 134400, 137664, 138688, 131264, 132288, 166336, 167377, 135360, 136384, 170368, 162048, 143680, 171411, 163087, 144704, 198662, 157952, 199713, 145472, 158989, 202752, 146503, 160128, 194624, 139264, 151680, 176256, 140292, 161152, 203790, 141411, 152704, 195658, 142400, 180767, 177285, 178176, 149504, 190550, 179223, 181760, 191576, 153856, 150557, 192585, 172032, 188928, 193630, 164160, 147456, 189980, 186368, 154891, 148480, 184328, 173076, 168192, 196608, 165200, 155648, 182272, 174080, 187419, 156672, 169228, 175104, 185344, 200722, 21, 183296, 197658, 25, 201760, 34, 0, 0, 0, 0, 0),
+    (137536, 138560, 133440, 134464, 170112, 135424, 136448, 171155, 131392, 132416, 145408, 166080, 155904, 146432, 167111, 156945, 139328, 168140, 159872, 140352, 169156, 18, 160896, 174592, 164110, 161792, 175616, 165141, 16, 162816, 143616, 188623, 158080, 144640, 189638, 28, 159104, 141376, 151552, 196749, 147712, 142400, 152576, 197765, 10, 192640, 153856, 176352, 148744, 154880, 190603, 184320, 202752, 177366, 193694, 149824, 191645, 185370, 203776, 180259, 194560, 150848, 186441, 195615, 198656, 181272, 178176, 199680, 187489, 27, 179200, 200704, 182295, 201728, 183330, 25, 172032, 173076, 0, 0),
+    (131392, 132416, 135488, 136512, 137472, 138496, 164032, 145472, 165056, 146512, 133440, 134471, 168320, 141312, 160000, 169362, 142341, 161024, 170446, 139584, 171456, 161811, 140612, 166336, 162816, 174159, 167377, 175168, 155797, 200832, 147456, 156812, 192640, 176128, 182272, 201890, 148480, 183304, 193689, 177152, 151582, 202880, 196630, 152586, 172032, 197632, 188448, 203939, 149504, 187008, 173076, 150528, 180233, 198656, 184320, 188059, 199713, 185344, 178202, 153600, 157952, 189468, 181272, 158989, 154624, 179211, 190464, 194583, 143360, 195615, 144390, 191517, 0, 0, 0, 0, 0, 0, 0, 0),
+    (135424, 136448, 137472, 138496, 139264, 168128, 140288, 169156, 131328, 132352, 133376, 134418, 143360, 170432, 161792, 144390, 171456, 162835, 172047, 164288, 155904, 153856, 165328, 156940, 173056, 166208, 191124, 154891, 167232, 192145, 141341, 202816, 160128, 142341, 203840, 161187, 178752, 157710, 196800, 194688, 147712, 158733, 188608, 195743, 179776, 186496, 184855, 148744, 197824, 176160, 174080, 189660, 200704, 145408, 182784, 198720, 185882, 175125, 187520, 177152, 151707, 183830, 199744, 201728, 146457, 192512, 149537, 34, 193536, 152711, 30, 180224, 150538, 9, 181272, 0, 0, 0, 0, 0),
+    (131328, 132352, 137344, 138368, 135488, 136512, 166336, 167377, 170368, 133568, 134592, 162048, 143680, 171411, 163087, 144704, 198662, 157952, 199680, 145505, 158989, 202752, 146503, 160128, 194624, 139264, 151680, 176256, 140292, 161152, 203790, 141411, 152704, 195658, 142400, 180767, 177285, 178176, 149504, 190550, 179223, 181760, 191576, 172032, 150557, 192585, 164160, 188928, 193630, 153856, 147456, 184320, 154891, 186368, 189952, 148508, 173056, 196616, 168212, 165184, 187392, 155648, 182288, 174107, 169234, 197632, 175136, 185344, 200725, 156672, 183322, 201740, 25, 34, 0, 0, 0, 0, 0, 0),
+    (131392, 132416, 137472, 138496, 135424, 136448, 170112, 171155, 133440, 134464, 166080, 143424, 155904, 167121, 144454, 156928, 168128, 174604, 159872, 169170, 175637, 160896, 164096, 141582, 161792, 165136, 142597, 162816, 188608, 151567, 158080, 189660, 152586, 159104, 196736, 153869, 192640, 197760, 154912, 11, 147712, 176320, 202752, 184320, 190592, 149824, 178176, 177344, 203798, 35, 193664, 191616, 150878, 29, 148736, 180224, 198656, 145417, 185344, 186432, 199688, 146458, 139264, 181248, 200737, 7, 179200, 187456, 172056, 194560, 182272, 201751, 27, 195584, 183330, 173087, 140313, 20, 4, 0),
+    (135424, 136448, 131392, 132416, 137536, 138560, 133440, 134464, 164032, 139328, 165056, 140368, 4, 168320, 160000, 169362, 161038, 170432, 141312, 161792, 171475, 142341, 182272, 166336, 174144, 162831, 167377, 151872, 183296, 200857, 175189, 155776, 192640, 152906, 187008, 201890, 176128, 156812, 193664, 147678, 177152, 188032, 202902, 196635, 172032, 143360, 188416, 197664, 203939, 180224, 184320, 144384, 173062, 178196, 157952, 198656, 148672, 189448, 28, 185344, 199680, 145690, 159009, 181261, 149528, 146695, 194560, 150528, 179209, 23, 153600, 190464, 195584, 154655, 11, 191517, 0, 0, 0, 0),
+    (133376, 134400, 135424, 136448, 168128, 131328, 132352, 162048, 169170, 163087, 137472, 138496, 170432, 139264, 191104, 171456, 140307, 4, 192128, 145664, 164317, 194688, 146695, 165328, 157696, 141312, 166208, 158733, 142336, 167237, 195712, 172032, 202833, 31, 147456, 203875, 184832, 173076, 196800, 143360, 176128, 148488, 188608, 200704, 178752, 186496, 144384, 185862, 179776, 197850, 153728, 177152, 174103, 189664, 154752, 201728, 182784, 198742, 151580, 175104, 187531, 160034, 199744, 152597, 183808, 192539, 33, 161024, 193546, 25, 155648, 180224, 149518, 156702, 181248, 150540, 24, 9, 0, 0),
+    (131200, 132224, 135360, 136384, 163904, 137408, 138432, 164944, 133248, 134272, 168000, 155776, 141376, 169042, 156812, 142400, 198661, 161920, 199680, 143457, 162959, 202752, 144454, 159872, 165888, 139264, 147584, 166929, 140292, 160896, 194638, 170048, 148616, 176256, 171091, 157824, 203811, 151552, 158861, 195648, 145439, 180736, 177302, 146439, 181760, 190552, 152576, 149514, 191552, 178205, 188928, 192576, 179223, 150537, 193600, 153694, 184320, 196608, 172032, 189980, 186368, 154699, 185370, 187392, 173083, 182272, 200724, 174080, 183321, 197632, 175136, 21, 201762, 0, 0, 0, 0, 0, 0, 0),
+    (137280, 138304, 135232, 136256, 131136, 132160, 163968, 143360, 133184, 134208, 165008, 144390, 170112, 172096, 159744, 171155, 145472, 160782, 168128, 146503, 155776, 169170, 173120, 156820, 166028, 176128, 139264, 167057, 149504, 188608, 177152, 140310, 189636, 150528, 157852, 196745, 151552, 158861, 174144, 152576, 192650, 197792, 202752, 184320, 175189, 178752, 193694, 190592, 179776, 147479, 191645, 203776, 185379, 186458, 148488, 198656, 187483, 194560, 180224, 199713, 141312, 182272, 200704, 195615, 183296, 201753, 142370, 181248, 161797, 153624, 162831, 154635, 0, 0, 0, 0, 0, 0, 0, 0),
+    (133184, 134208, 131136, 132160, 135232, 136256, 137280, 138304, 168128, 145472, 169152, 146514, 7, 163968, 143424, 157696, 164992, 144464, 6, 147584, 169984, 139328, 158733, 171008, 140371, 148612, 166080, 141384, 159744, 167104, 142417, 5, 151552, 200832, 180800, 160782, 192640, 153600, 152586, 201856, 176674, 155776, 193664, 154654, 11, 156800, 202880, 177676, 22, 149632, 203904, 181859, 150680, 198656, 196617, 161920, 199680, 197665, 32, 172032, 184320, 182848, 162959, 185344, 183898, 173081, 186900, 190464, 188416, 187931, 189468, 194560, 178176, 174080, 195615, 191517, 175125, 179223, 0, 0),
+    (135168, 136192, 133120, 134144, 166080, 141312, 155776, 131072, 132096, 167104, 142353, 156800, 137216, 138245, 139264, 168128, 159884, 140292, 169152, 160914, 143360, 164046, 161792, 144390, 165056, 162832, 145408, 194639, 157824, 146439, 195648, 158879, 176704, 170189, 180352, 153600, 171219, 181400, 177728, 202816, 186902, 154635, 203840, 187939, 151552, 178267, 184832, 152586, 196800, 172032, 147456, 179287, 185882, 148480, 197824, 173064, 32, 174080, 198720, 200724, 149504, 199777, 182912, 175125, 183961, 150537, 201762, 192512, 188416, 189468, 190464, 193566, 191517, 0, 0, 0, 0, 0, 0, 0),
 )
 
 
@@ -32,41 +53,55 @@
     key_tile = window[back, head, 0]
     value_tile = window[back, head, 1]
     iota = lax.broadcasted_iota(jnp.int32, (TILE, TOK), 0)
+    seen = []
+    for half in range(2):
+        mask = iota >= thresholds[pl.ds(back * 2 + half, 1), :]
+        if own:
+            mask = mask & (iota + half * TILE <= lax.broadcasted_iota(jnp.int32, (TILE, TOK), 1))
+        seen.append(mask)
+    spans = [slice(member * TOK, (member + 1) * TOK) for member in range(GROUP)]
+    if not own:
+        old_tops = [top[head, :, span] for span in spans]
+        old_totals = [total[head, :, span] for span in spans]
+    raw = [
+        jnp.dot(key_tile, queries_t[head, :, span], preferred_element_type=jnp.float32)
+        for span in spans
+    ]
+    tops, totals, factors, products = [], [], [], []
     for member in range(GROUP):
-        span = slice(member * TOK, (member + 1) * TOK)
-        scores = jnp.dot(
-            key_tile, queries_t[head, :, span], preferred_element_type=jnp.float32
-        )
-        halves = []
-        for half in range(2):
-            low = thresholds[pl.ds(back * 2 + half, 1), :]
-            seen = iota >= low
-            if own:
-                seen = seen & (
-                    iota + half * TILE <= lax.broadcasted_iota(jnp.int32, (TILE, TOK), 1)
-                )
-            halves.append(jnp.where(seen, scores[half * TILE : (half + 1) * TILE], NEG))
-        scores = jnp.concatenate(halves, axis=0)
+        scores = jnp.concatenate(
+            [
+                jnp.where(seen[half], raw[member][half * TILE : (half + 1) * TILE], NEG)
+                for half in range(2)
+            ],
+            axis=0,
+        )
         new_top = jnp.max(scores, axis=0, keepdims=True)
         if not own:
-            old_top = top[head, :, span]
-            new_top = jnp.maximum(old_top, new_top)
+            new_top = jnp.maximum(old_tops[member], new_top)
         scaled_top = new_top * scale
         weights = jnp.exp2(scores * scale - scaled_top)
         weight_sum = jnp.sum(weights, axis=0, keepdims=True)
-        product = lax.dot_general(
-            value_tile,
-            weights.astype(jnp.bfloat16),
-            (((0,), (0,)), ((), ())),
-            preferred_element_type=jnp.float32,
+        products.append(
+            lax.dot_general(
+                value_tile,
+                weights.astype(jnp.bfloat16),
+                (((0,), (0,)), ((), ())),
+                preferred_element_type=jnp.float32,
+            )
         )
         if not own:
-            factor = jnp.exp2(old_top * scale - scaled_top)
-            weight_sum = total[head, :, span] * factor + weight_sum
-            product = summed[head, :, span] * factor + product
-        top[head, :, span] = new_top
-        total[head, :, span] = weight_sum
-        summed[head, :, span] = product
+            factors.append(jnp.exp2(old_tops[member] * scale - scaled_top))
+            weight_sum = old_totals[member] * factors[member] + weight_sum
+        tops.append(new_top)
+        totals.append(weight_sum)
+    for member, span in enumerate(spans):
+        top[head, :, span] = tops[member]
+        total[head, :, span] = totals[member]
+        if own:
+            summed[head, :, span] = products[member]
+        else:
+            summed[head, :, span] = summed[head, :, span] * factors[member] + products[member]
 
 
 def kernel(
@@ -110,11 +145,21 @@
         -SIDE,
     )
 
+    row = seq // SIDE
+    rows = devices // SIDE
+    not_last = row < rows - 1
+    not_first = row > 0
+
     barrier = pltpu.get_barrier_semaphore()
-    for where in neighbours:
-        pl.semaphore_signal(
-            barrier, inc=1, device_id=(where, core), device_id_type=MESH
-        )
+    for where, there in zip(neighbours, (None, None, not_last, not_first)):
+
+        def greet(where=where):
+            pl.semaphore_signal(barrier, inc=1, device_id=(where, core), device_id_type=MESH)
+
+        if there is None:
+            greet()
+        else:
+            pl.when(there)(greet)
     pl.semaphore_signal(barrier, inc=1, device_id=(seq, 1 - core), device_id_type=MESH)
 
     locals_ = []
@@ -128,7 +173,9 @@
         )
     for copy in locals_:
         copy.start()
-    pl.semaphore_wait(barrier, 5)
+    pl.semaphore_wait(
+        barrier, 3 + jnp.where(not_last, 1, 0) + jnp.where(not_first, 1, 0)
+    )
     swaps = []
     for part, ref in enumerate((k_ref, v_ref)):
         swaps.append(
@@ -185,25 +232,34 @@
             device_id_type=MESH,
         )
 
+    kind = jnp.where(
+        row == rows - 1,
+        5 * SIDE,
+        jnp.where(row == rows - 2, 4 * SIDE, lax.rem(row, SIDE) * SIDE),
+    )
+    kind = kind + place
+    steps = len(PLAN[0])
     words = []
-    for j in range(ENTRIES // 3):
-        word = PLAN[0][j]
-        for c in range(1, SIDE):
-            word = jnp.where(place == c, PLAN[c][j], word)
+    for n in range(steps):
+        word = PLAN[0][n]
+        for c in range(1, len(PLAN)):
+            word = jnp.where(kind == c, PLAN[c][n], word)
         words.append(word)
 
-    def entry(n):
-        j, third = n // 3, lax.rem(n, 3)
-        word = words[0]
-        for i in range(1, ENTRIES // 3):
-            word = jnp.where(j == i, words[i], word)
-        divisor = jnp.where(third == 0, 1, jnp.where(third == 1, 1024, 1048576))
-        code = lax.rem(word // divisor, 1024)
-        return code // 16, lax.rem(code, 16)
-
-    def relay(slot, directions):
-        for part in range(2):
-
+    def word_of(turn, place_in_turn):
+        word = words[place_in_turn]
+        for i in range(1, steps // TURN):
+            word = jnp.where(turn == i, words[i * TURN + place_in_turn], word)
+        return word
+
+    def relay(code):
+        slot = lax.rem(code // 32, 64)
+        part = lax.rem(code // 16, 2)
+        directions = lax.rem(code, 16)
+        back = slot // HEADS
+
+        @pl.when((code >= 2048) & (back <= seq))
+        def _():
             @pl.when(slot >= HEADS)
             def _():
                 arrived(slot, part).wait_recv()
@@ -213,6 +269,19 @@
                 @pl.when(lax.rem(directions // (1 << direction), 2) == 1)
                 def _():
                     hand_on(slot, part, direction).start()
+
+    def sent(code):
+        slot = lax.rem(code // 32, 64)
+        part = lax.rem(code // 16, 2)
+        directions = lax.rem(code, 16)
+
+        @pl.when((code >= 2048) & (slot // HEADS <= seq))
+        def _():
+            for direction in range(4):
+
+                @pl.when(lax.rem(directions // (1 << direction), 2) == 1)
+                def _():
+                    hand_on(slot, part, direction).wait_send()
 
     for copy in locals_:
         copy.wait()
@@ -220,22 +289,28 @@
         copy.wait()
 
     for n in range(FIRST):
-        relay(*entry(n))
+        relay(words[n] // 64)
     for head in range(HEADS):
         attend(queries_t, window, thresholds, top, total, summed, 0, head, True)
 
-    def step(n, _):
-        slot, directions = entry(n)
-        relay(slot, directions)
-
-        @pl.when(slot >= HEADS)
-        def _():
-            back, head = slot // HEADS, lax.rem(slot, HEADS)
-            attend(queries_t, window, thresholds, top, total, summed, back, head, False)
+    def step(turn, _):
+        for place_in_turn in range(TURN):
+            word = word_of(turn, place_in_turn)
+
+            @pl.when(turn * TURN + place_in_turn >= FIRST)
+            def _():
+                relay(word // 64)
+
+            slot = lax.rem(word, 64)
+
+            @pl.when((slot >= HEADS) & (slot // HEADS <= seq))
+            def _():
+                back, head = slot // HEADS, lax.rem(slot, HEADS)
+                attend(queries_t, window, thresholds, top, total, summed, back, head, False)
 
         return 0
 
-    lax.fori_loop(FIRST, ENTRIES, step, 0)
+    lax.fori_loop(0, steps // TURN, step, 0)
 
     for head in range(HEADS):
         for member in range(GROUP):
@@ -244,18 +319,12 @@
             result[:, head * GROUP + member, :] = (summed[head, :, span] * inverse).T
     o_ref[...] = result[...].astype(jnp.bfloat16)
 
-    def finish(n, _):
-        slot, directions = entry(n)
-        for part in range(2):
-            for direction in range(4):
-
-                @pl.when(lax.rem(directions // (1 << direction), 2) == 1)
-                def _():
-                    hand_on(slot, part, direction).wait_send()
-
+    def finish(turn, _):
+        for place_in_turn in range(TURN):
+            sent(word_of(turn, place_in_turn) // 64)
         return 0
 
-    lax.fori_loop(0, ENTRIES, finish, 0)
+    lax.fori_loop(0, steps // TURN, finish, 0)
 
 
 def body(queries, keys, values, doc_start, tile_list, tile_count):

time: 82.5 us -> 63.4 us (0.77)
  the two profiles are of different devices: /device:TPU:1 before, /device:TPU:226 now
where the time goes in v1:
time: 63.4 us; the launch traced here: 63.1 us
  Pallas kernels  58.1 us (92%)
  local copies, waits for them, and re-layouts  4.29 us (7%)
  between operations  0.66 us (1%)
    pallas_call x1, Pallas kernels, body(): pl.pallas_call(kernel, out_shape=jax.ShapeDtypeStruct(queries.shape, jnp....  58.1 us
    unnamed x1, local copies, waits for them, and re-layouts  2.37 us
    transpose x1, local copies, waits for them, and re-layouts, body(): values_t = jnp.swapaxes(values, 0, 1)  1.92 us

profile of v1, /device:TPU:226, one launch (start us, length us, event | category | flops | bytes accessed | tf_op | source)
XLA Modules:
  0.0 63.1 jit_solution(15958730148421792314)
XLA Ops:
  0.7 1.9 %copy_bitcast_fusion = (bf16[8,128,128]{2,1,0:T(8,128)(2,1)}, bf16[8,128,128]{2,1,0:T(8,128)(2,1)}) fusion(bf16[128,8,128]{2,1,0:T(8,128)(2,1)} %param.8, bf16[128,8,128]{2,1,0:T(8,128)(2,1)} %param.7), kind=kLoop, calls=%fused_computation | loop fusion | bytes 1048576 | tf_op jit(solution)/shard_map/transpose | solution.py:332
  2.6 58.1 %shard_map.64 = bf16[256,16,128]{2,1,0:T(8,128)(2,1)} custom-call(bf16[256,16,128]{2,1,0:T(8,128)(2,1)} %q_ref.1, bf16[8,128,128]{2,1,0:T(8,128)(2,1)} %get-tuple-element.6.k_ref, bf16[8,128,128]{2,1,0:T(8,128)(2,1)} %get-tuple-element.5.v_ref, s32[1,256]{1,0:T(1,128)} %bitcast.5, s32[1,18]{1,0:T(1,128)} %list_ref.1, s32[1]{0:T(128)S(6)} %copy.12.count_ref), custom_call_target="tpu_custom_call" | custom-call | tf_op jit(solution)/shard_map/pallas_call | solution.py:336
  60.7 2.4 %copy.13 = bf16[256,16,128]{2,1,0:T(8,128)(2,1)} copy(bf16[256,16,128]{2,1,0:T(8,128)(2,1)} %shard_map.64) | data formatting | bytes 2097152

commit v2 on v1

--- a/solution.py
+++ b/solution.py
@@ -16,6 +16,7 @@
 ENTRIES = BACK * HEADS
 FIRST = 2
 TURN = 5
+LAG = 3
 NEG = -1e30
 FAR = 1 << 20
 MESH = pl.DeviceIdType.MESH
@@ -119,7 +120,12 @@
     total,
     summed,
     result,
-    local_sem,
+    q_here,
+    kv_here,
+    swapped,
+    o_here,
+    in_sem,
+    out_sem,
     swap_send,
     swap_recv,
     send_sem,
@@ -160,77 +166,14 @@
             greet()
         else:
             pl.when(there)(greet)
-    pl.semaphore_signal(barrier, inc=1, device_id=(seq, 1 - core), device_id_type=MESH)
-
-    locals_ = []
-    for part, ref in enumerate((k_ref, v_ref)):
-        locals_.append(
-            pltpu.make_async_copy(
-                ref.at[pl.ds(core * HEADS, HEADS)],
-                window.at[0, :, part, pl.ds(core * TILE, TILE), :],
-                local_sem.at[part],
-            )
-        )
-    for copy in locals_:
+
+    ins = []
+    for part, (ref, here) in enumerate(
+        ((k_ref, kv_here.at[0]), (v_ref, kv_here.at[1]), (q_ref, q_here))
+    ):
+        ins.append(pltpu.make_async_copy(ref, here, in_sem.at[part]))
+    for copy in ins:
         copy.start()
-    pl.semaphore_wait(
-        barrier, 3 + jnp.where(not_last, 1, 0) + jnp.where(not_first, 1, 0)
-    )
-    swaps = []
-    for part, ref in enumerate((k_ref, v_ref)):
-        swaps.append(
-            pltpu.make_async_remote_copy(
-                src_ref=ref.at[pl.ds((1 - core) * HEADS, HEADS)],
-                dst_ref=window.at[0, :, part, pl.ds(core * TILE, TILE), :],
-                send_sem=swap_send.at[part],
-                recv_sem=swap_recv.at[part],
-                device_id=(seq, 1 - core),
-                device_id_type=MESH,
-            )
-        )
-    for copy in swaps:
-        copy.start()
-
-    tile_row = lax.broadcasted_iota(jnp.int32, (24, 1), 0)
-    back_of = tile_row // 2
-    half_of = tile_row - 2 * back_of
-    tile_id = 2 * (seq - back_of) + half_of
-    slots = list_ref.shape[1]
-    listed = (list_ref[...] == tile_id) & (
-        lax.broadcasted_iota(jnp.int32, (1, slots), 1) < count_ref[0]
-    )
-    live = jnp.max(jnp.where(listed, 1.0, 0.0), axis=1, keepdims=True)
-    low = start_ref[...] - seq * TOK + (back_of * TOK - half_of * TILE)
-    thresholds[...] = jnp.where(live > 0.5, low, FAR)
-
-    for head in range(HEADS):
-        for member in range(GROUP):
-            queries_t[head, :, member * TOK : (member + 1) * TOK] = q_ref[
-                :, head * GROUP + member, :
-            ].T
-
-    def hand_on(slot, part, direction):
-        back, head = slot // HEADS, lax.rem(slot, HEADS)
-        there = back + shifts[direction]
-        return pltpu.make_async_remote_copy(
-            src_ref=window.at[back, head, part],
-            dst_ref=window.at[there, head, part],
-            send_sem=send_sem.at[slot, part, direction],
-            recv_sem=recv_sem.at[there * HEADS + head, part],
-            device_id=(neighbours[direction], core),
-            device_id_type=MESH,
-        )
-
-    def arrived(slot, part):
-        back, head = slot // HEADS, lax.rem(slot, HEADS)
-        return pltpu.make_async_remote_copy(
-            src_ref=window.at[back, head, part],
-            dst_ref=window.at[back, head, part],
-            send_sem=send_sem.at[slot, part, 0],
-            recv_sem=recv_sem.at[slot, part],
-            device_id=(neighbours[0], core),
-            device_id_type=MESH,
-        )
 
     kind = jnp.where(
         row == rows - 1,
@@ -252,54 +195,124 @@
             word = jnp.where(turn == i, words[i * TURN + place_in_turn], word)
         return word
 
-    def relay(code):
+    tile_row = lax.broadcasted_iota(jnp.int32, (24, 1), 0)
+    back_of = tile_row // 2
+    half_of = tile_row - 2 * back_of
+    tile_id = 2 * (seq - back_of) + half_of
+    slots = list_ref.shape[1]
+    listed = (list_ref[...] == tile_id) & (
+        lax.broadcasted_iota(jnp.int32, (1, slots), 1) < count_ref[0]
+    )
+    live = jnp.max(jnp.where(listed, 1.0, 0.0), axis=1, keepdims=True)
+    low = start_ref[...] - seq * TOK + (back_of * TOK - half_of * TILE)
+    thresholds[...] = jnp.where(live > 0.5, low, FAR)
+    for part in range(2):
+        ins[part].wait()
+        for mine in range(2):
+
+            @pl.when(core == mine)
+            def _():
+                for head in range(HEADS):
+                    window[0, head, part, mine * TILE : (mine + 1) * TILE, :] = kv_here[
+                        part, :, mine * HEADS + head, :
+                    ]
+                    swapped[part, head] = kv_here[part, :, (1 - mine) * HEADS + head, :]
+
+    pl.semaphore_signal(barrier, inc=1, device_id=(seq, 1 - core), device_id_type=MESH)
+    pl.semaphore_wait(
+        barrier, 3 + jnp.where(not_last, 1, 0) + jnp.where(not_first, 1, 0)
+    )
+    swaps = []
+    for part in range(2):
+        swaps.append(
+            pltpu.make_async_remote_copy(
+                src_ref=swapped.at[part],
+                dst_ref=window.at[0, :, part, pl.ds(core * TILE, TILE), :],
+                send_sem=swap_send.at[part],
+                recv_sem=swap_recv.at[part],
+                device_id=(seq, 1 - core),
+                device_id_type=MESH,
+            )
+        )
+    for copy in swaps:
+        copy.start()
+
+    ins[2].wait()
+    for head in range(HEADS):
+        for member in range(GROUP):
+            queries_t[head, :, member * TOK : (member + 1) * TOK] = q_here[
+                :, head * GROUP + member, :
+            ].T
+
+    def hand_on(n, back, head, part, direction):
+        there = back + shifts[direction]
+        return pltpu.make_async_remote_copy(
+            src_ref=window.at[back, head, part],
+            dst_ref=window.at[there, head, part],
+            send_sem=send_sem.at[n, direction],
+            recv_sem=recv_sem.at[there * HEADS + head, part],
+            device_id=(neighbours[direction], core),
+            device_id_type=MESH,
+        )
+
+    def wait_for(n, back, head, part, direction):
+        return pltpu.make_async_remote_copy(
+            src_ref=window.at[back, head, part],
+            dst_ref=window.at[back, head, part],
+            send_sem=send_sem.at[n, direction],
+            recv_sem=recv_sem.at[back * HEADS + head, part],
+            device_id=(neighbours[0], core),
+            device_id_type=MESH,
+        )
+
+    def relay(n, code):
         slot = lax.rem(code // 32, 64)
         part = lax.rem(code // 16, 2)
         directions = lax.rem(code, 16)
-        back = slot // HEADS
+        back, head = slot // HEADS, lax.rem(slot, HEADS)
 
         @pl.when((code >= 2048) & (back <= seq))
         def _():
             @pl.when(slot >= HEADS)
             def _():
-                arrived(slot, part).wait_recv()
+                wait_for(n, back, head, part, 0).wait_recv()
 
             for direction in range(4):
 
                 @pl.when(lax.rem(directions // (1 << direction), 2) == 1)
                 def _():
-                    hand_on(slot, part, direction).start()
-
-    def sent(code):
+                    hand_on(n, back, head, part, direction).start()
+
+    def sent(n, code):
         slot = lax.rem(code // 32, 64)
         part = lax.rem(code // 16, 2)
         directions = lax.rem(code, 16)
-
-        @pl.when((code >= 2048) & (slot // HEADS <= seq))
+        back, head = slot // HEADS, lax.rem(slot, HEADS)
+
+        @pl.when((directions > 0) & (back <= seq))
         def _():
             for direction in range(4):
 
                 @pl.when(lax.rem(directions // (1 << direction), 2) == 1)
                 def _():
-                    hand_on(slot, part, direction).wait_send()
-
-    for copy in locals_:
-        copy.wait()
+                    wait_for(n, back, head, part, direction).wait_send()
+
     for copy in swaps:
         copy.wait()
 
     for n in range(FIRST):
-        relay(words[n] // 64)
+        relay(n, words[n] // 64)
     for head in range(HEADS):
         attend(queries_t, window, thresholds, top, total, summed, 0, head, True)
 
     def step(turn, _):
         for place_in_turn in range(TURN):
+            n = turn * TURN + place_in_turn
             word = word_of(turn, place_in_turn)
 
-            @pl.when(turn * TURN + place_in_turn >= FIRST)
+            @pl.when(n >= FIRST)
             def _():
-                relay(word // 64)
+                relay(n, word // 64)
 
             slot = lax.rem(word, 64)
 
@@ -308,36 +321,49 @@
                 back, head = slot // HEADS, lax.rem(slot, HEADS)
                 attend(queries_t, window, thresholds, top, total, summed, back, head, False)
 
+            @pl.when(turn >= LAG)
+            def _():
+                sent(n - LAG * TURN, word_of(turn - LAG, place_in_turn) // 64)
+
         return 0
 
     lax.fori_loop(0, steps // TURN, step, 0)
 
-    for head in range(HEADS):
-        for member in range(GROUP):
-            span = slice(member * TOK, (member + 1) * TOK)
-            inverse = 1.0 / total[head, :, span]
-            result[:, head * GROUP + member, :] = (summed[head, :, span] * inverse).T
-    o_ref[...] = result[...].astype(jnp.bfloat16)
+    outs = []
+    for half in range(2):
+        rows_out = slice(half * 128, (half + 1) * 128)
+        for head in range(HEADS):
+            for member in range(GROUP):
+                span = slice(member * TOK + half * 128, member * TOK + (half + 1) * 128)
+                inverse = 1.0 / total[head, :, span]
+                result[rows_out, head * GROUP + member, :] = (summed[head, :, span] * inverse).T
+        o_here[rows_out] = result[rows_out].astype(jnp.bfloat16)
+        outs.append(
+            pltpu.make_async_copy(o_here.at[rows_out], o_ref.at[rows_out], out_sem.at[half])
+        )
+        if half > 0:
+            outs[half - 1].start()
+    outs[-1].start()
 
     def finish(turn, _):
         for place_in_turn in range(TURN):
-            sent(word_of(turn, place_in_turn) // 64)
+            sent(turn * TURN + place_in_turn, word_of(turn, place_in_turn) // 64)
         return 0
 
-    lax.fori_loop(0, steps // TURN, finish, 0)
+    lax.fori_loop(steps // TURN - LAG, steps // TURN, finish, 0)
+    for copy in outs:
+        copy.wait()
 
 
 def body(queries, keys, values, doc_start, tile_list, tile_count):
-    keys_t = jnp.swapaxes(keys, 0, 1)
-    values_t = jnp.swapaxes(values, 0, 1)
     vmem = pl.BlockSpec(memory_space=pltpu.VMEM)
     hbm = pl.BlockSpec(memory_space=pltpu.HBM)
     lanes = GROUP * TOK
     return pl.pallas_call(
         kernel,
         out_shape=jax.ShapeDtypeStruct(queries.shape, jnp.bfloat16),
-        in_specs=[vmem, hbm, hbm, vmem, vmem, pl.BlockSpec(memory_space=pltpu.SMEM)],
-        out_specs=vmem,
+        in_specs=[hbm, hbm, hbm, vmem, vmem, pl.BlockSpec(memory_space=pltpu.SMEM)],
+        out_specs=hbm,
         scratch_shapes=[
             pltpu.VMEM((BACK, HEADS, 2, TOK, HD), jnp.bfloat16),
             pltpu.VMEM((HEADS, HD, lanes), jnp.bfloat16),
@@ -346,14 +372,19 @@
             pltpu.VMEM((HEADS, 1, lanes), jnp.float32),
             pltpu.VMEM((HEADS, HD, lanes), jnp.float32),
             pltpu.VMEM(queries.shape, jnp.float32),
+            pltpu.VMEM(queries.shape, jnp.bfloat16),
+            pltpu.VMEM((2, TILE, 2 * HEADS, HD), jnp.bfloat16),
+            pltpu.VMEM((2, HEADS, TILE, HD), jnp.bfloat16),
+            pltpu.VMEM(queries.shape, jnp.bfloat16),
+            pltpu.SemaphoreType.DMA((3,)),
             pltpu.SemaphoreType.DMA((2,)),
             pltpu.SemaphoreType.DMA((2,)),
             pltpu.SemaphoreType.DMA((2,)),
-            pltpu.SemaphoreType.DMA((ENTRIES, 2, 4)),
+            pltpu.SemaphoreType.DMA((len(PLAN[0]), 4)),
             pltpu.SemaphoreType.DMA((ENTRIES, 2)),
         ],
         compiler_params=pltpu.CompilerParams(collective_id=0, has_side_effects=True),
-    )(queries, keys_t, values_t, doc_start.reshape(1, TOK), tile_list, tile_count)
+    )(queries, keys, values, doc_start.reshape(1, TOK), tile_list, tile_count)
 
 
 def solution(mesh):

time: 63.4 us -> 62.1 us (0.979)
  local copies, waits for them, and re-layouts: 4.29 us -> 2.37 us
  Pallas kernels: 58.1 us -> 58.9 us
    transpose x1 -> x0, local copies, waits for them, and re-layouts: 1.92 us -> none  [body(): values_t = jnp.swapaxes(values, 0, 1)]
    pallas_call x1, Pallas kernels: 58.1 us -> 58.9 us  [body(): pl.pallas_call(kernel, out_shape=jax.ShapeDtypeStruct(queries.shape, jnp....]
where the time goes in v2:
time: 62.1 us; the launch traced here: 61.9 us
  Pallas kernels  58.9 us (95%)
  local copies, waits for them, and re-layouts  2.37 us (4%)
  between operations  0.66 us (1%)
    pallas_call x1, Pallas kernels, body(): pl.pallas_call(kernel, out_shape=jax.ShapeDtypeStruct(queries.shape, jnp....  58.9 us
    unnamed x1, local copies, waits for them, and re-layouts  2.37 us

profile of v2, /device:TPU:226, one launch (start us, length us, event | category | flops | bytes accessed | tf_op | source)
XLA Modules:
  0.0 61.9 jit_solution(17136842435458050170)
XLA Ops:
  0.7 58.9 %shard_map.64 = bf16[256,16,128]{2,1,0:T(8,128)(2,1)} custom-call(bf16[256,16,128]{2,1,0:T(8,128)(2,1)} %q_ref.1, bf16[128,8,128]{2,1,0:T(8,128)(2,1)} %k_ref.1, bf16[128,8,128]{2,1,0:T(8,128)(2,1)} %v_ref.1, s32[1,256]{1,0:T(1,128)} %bitcast.1, s32[1,18]{1,0:T(1,128)} %list_ref.1, s32[1]{0:T(128)S(6)} %copy.8.count_ref), custom_call_target="tpu_custom_call" | custom-call | tf_op jit(solution)/shard_map/pallas_call | solution.py:362
  59.6 2.4 %copy.9 = bf16[256,16,128]{2,1,0:T(8,128)(2,1)} copy(bf16[256,16,128]{2,1,0:T(8,128)(2,1)} %shard_map.64) | data formatting | bytes 2097152

commit v3 on v2

--- a/solution.py
+++ b/solution.py
@@ -15,8 +15,8 @@
 HD = 128
 ENTRIES = BACK * HEADS
 FIRST = 2
-TURN = 5
-LAG = 3
+TURN = 10
+LAG = 2
 NEG = -1e30
 FAR = 1 << 20
 MESH = pl.DeviceIdType.MESH

time: 62.1 us -> 59.7 us (0.961)
  Pallas kernels: 58.9 us -> 56.5 us
    pallas_call x1, Pallas kernels: 58.9 us -> 56.5 us  [body(): pl.pallas_call(kernel, out_shape=jax.ShapeDtypeStruct(queries.shape, jnp....]
where the time goes in v3:
time: 59.7 us; the launch traced here: 59.5 us
  Pallas kernels  56.5 us (95%)
  local copies, waits for them, and re-layouts  2.37 us (4%)
  between operations  0.66 us (1%)
    pallas_call x1, Pallas kernels, body(): pl.pallas_call(kernel, out_shape=jax.ShapeDtypeStruct(queries.shape, jnp....  56.5 us
    unnamed x1, local copies, waits for them, and re-layouts  2.37 us

profile of v3, /device:TPU:226, one launch (start us, length us, event | category | flops | bytes accessed | tf_op | source)
XLA Modules:
  0.0 59.5 jit_solution(1364400903575526377)
XLA Ops:
  0.7 56.5 %shard_map.64 = bf16[256,16,128]{2,1,0:T(8,128)(2,1)} custom-call(bf16[256,16,128]{2,1,0:T(8,128)(2,1)} %q_ref.1, bf16[128,8,128]{2,1,0:T(8,128)(2,1)} %k_ref.1, bf16[128,8,128]{2,1,0:T(8,128)(2,1)} %v_ref.1, s32[1,256]{1,0:T(1,128)} %bitcast.1, s32[1,18]{1,0:T(1,128)} %list_ref.1, s32[1]{0:T(128)S(6)} %copy.8.count_ref), custom_call_target="tpu_custom_call" | custom-call | tf_op jit(solution)/shard_map/pallas_call | solution.py:362
  57.1 2.4 %copy.9 = bf16[256,16,128]{2,1,0:T(8,128)(2,1)} copy(bf16[256,16,128]{2,1,0:T(8,128)(2,1)} %shard_map.64) | data formatting | bytes 2097152

commit v4 on v3

--- a/solution.py
+++ b/solution.py
@@ -123,9 +123,7 @@
     q_here,
     kv_here,
     swapped,
-    o_here,
     in_sem,
-    out_sem,
     swap_send,
     swap_recv,
     send_sem,
@@ -329,7 +327,6 @@
 
     lax.fori_loop(0, steps // TURN, step, 0)
 
-    outs = []
     for half in range(2):
         rows_out = slice(half * 128, (half + 1) * 128)
         for head in range(HEADS):
@@ -337,13 +334,7 @@
                 span = slice(member * TOK + half * 128, member * TOK + (half + 1) * 128)
                 inverse = 1.0 / total[head, :, span]
                 result[rows_out, head * GROUP + member, :] = (summed[head, :, span] * inverse).T
-        o_here[rows_out] = result[rows_out].astype(jnp.bfloat16)
-        outs.append(
-            pltpu.make_async_copy(o_here.at[rows_out], o_ref.at[rows_out], out_sem.at[half])
-        )
-        if half > 0:
-            outs[half - 1].start()
-    outs[-1].start()
+        o_ref[rows_out] = result[rows_out].astype(jnp.bfloat16)
 
     def finish(turn, _):
         for place_in_turn in range(TURN):
@@ -351,8 +342,6 @@
         return 0
 
     lax.fori_loop(steps // TURN - LAG, steps // TURN, finish, 0)
-    for copy in outs:
-        copy.wait()
 
 
 def body(queries, keys, values, doc_start, tile_list, tile_count):
@@ -363,7 +352,7 @@
         kernel,
         out_shape=jax.ShapeDtypeStruct(queries.shape, jnp.bfloat16),
         in_specs=[hbm, hbm, hbm, vmem, vmem, pl.BlockSpec(memory_space=pltpu.SMEM)],
-        out_specs=hbm,
+        out_specs=vmem,
         scratch_shapes=[
             pltpu.VMEM((BACK, HEADS, 2, TOK, HD), jnp.bfloat16),
             pltpu.VMEM((HEADS, HD, lanes), jnp.bfloat16),
@@ -375,15 +364,15 @@
             pltpu.VMEM(queries.shape, jnp.bfloat16),
             pltpu.VMEM((2, TILE, 2 * HEADS, HD), jnp.bfloat16),
             pltpu.VMEM((2, HEADS, TILE, HD), jnp.bfloat16),
-            pltpu.VMEM(queries.shape, jnp.bfloat16),
             pltpu.SemaphoreType.DMA((3,)),
-            pltpu.SemaphoreType.DMA((2,)),
             pltpu.SemaphoreType.DMA((2,)),
             pltpu.SemaphoreType.DMA((2,)),
             pltpu.SemaphoreType.DMA((len(PLAN[0]), 4)),
             pltpu.SemaphoreType.DMA((ENTRIES, 2)),
         ],
-        compiler_params=pltpu.CompilerParams(collective_id=0, has_side_effects=True),
+        compiler_params=pltpu.CompilerParams(
+            collective_id=0, has_side_effects=True, vmem_limit_bytes=32 * 1024 * 1024
+        ),
     )(queries, keys, values, doc_start.reshape(1, TOK), tile_list, tile_count)
 
 

time: 59.7 us -> 61.3 us (1.027)
  local copies, waits for them, and re-layouts: 2.37 us -> 4.76 us
  Pallas kernels: 56.5 us -> 55.6 us
    unnamed x1 -> x11, local copies, waits for them, and re-layouts: 2.37 us -> 4.76 us
    pallas_call x1, Pallas kernels: 56.5 us -> 55.6 us  [body(): pl.pallas_call(kernel, out_shape=jax.ShapeDtypeStruct(queries.shape, jnp....]
where the time goes in v4:
time: 61.3 us; the launch traced here: 61.1 us
  Pallas kernels  55.6 us (91%)
  local copies, waits for them, and re-layouts  4.76 us (8%)
  between operations  0.68 us (1%)
    pallas_call x1, Pallas kernels, body(): pl.pallas_call(kernel, out_shape=jax.ShapeDtypeStruct(queries.shape, jnp....  55.6 us
    unnamed x11, local copies, waits for them, and re-layouts  4.76 us

profile of v4, /device:TPU:226, one launch (start us, length us, event | category | flops | bytes accessed | tf_op | source)
XLA Modules:
  0.0 61.1 jit_solution(2580159107964171793)
XLA Ops:
  0.7 0.0 copy-start.3
  0.7 0.0 copy-start.4
  0.7 0.7 %copy-done.3 = s32[256]{0:T(256)S(1)} copy-done((s32[256]{0:T(256)S(1)}, s32[256]{0:T(256)}, u32[]{:S(2)}) %copy-start.3) | copy-done | bytes 1048
  1.3 0.0 copy-done.4
  1.3 0.0 copy-start
  1.3 1.2 %copy-done = bf16[256,16,128]{2,1,0:T(8,128)(2,1)S(1)} copy-done((bf16[256,16,128]{2,1,0:T(8,128)(2,1)S(1)}, bf16[256,16,128]{2,1,0:T(8,128)(2,1)}, u32[]{:S(2)}) %copy-start) | copy-done | bytes 1048600
  2.6 0.0 copy-start.1
  2.6 0.9 %copy-done.1 = bf16[128,8,128]{2,1,0:T(8,128)(2,1)S(1)} copy-done((bf16[128,8,128]{2,1,0:T(8,128)(2,1)S(1)}, bf16[128,8,128]{2,1,0:T(8,128)(2,1)}, u32[]{:S(2)}) %copy-start.1) | copy-done | bytes 262168
  3.5 0.0 copy-start.2
  3.5 0.9 %copy-done.2 = bf16[128,8,128]{2,1,0:T(8,128)(2,1)S(1)} copy-done((bf16[128,8,128]{2,1,0:T(8,128)(2,1)S(1)}, bf16[128,8,128]{2,1,0:T(8,128)(2,1)}, u32[]{:S(2)}) %copy-start.2) | copy-done | bytes 262168
  4.5 55.6 %shard_map.64 = bf16[256,16,128]{2,1,0:T(8,128)(2,1)S(1)} custom-call(bf16[256,16,128]{2,1,0:T(8,128)(2,1)S(1)} %copy-done, bf16[128,8,128]{2,1,0:T(8,128)(2,1)S(1)} %copy-done.1, bf16[128,8,128]{2,1,0:T(8,128)(2,1)S(1)} %copy-done.2, s32[1,256]{1,0:T(1,128)S(1)} %bitcast.1, s32[1,18]{1,0:T(1,128)S(1)} %copy-done.4, s32[1]{0:T(128)S(6)} %copy.8.count_ref), custom_call_target="tpu_custom_call" | custom-call | tf_op jit(solution)/shard_map/pallas_call | solution.py:351
  60.1 1.0 %copy.9 = bf16[256,16,128]{2,1,0:T(8,128)(2,1)} copy(bf16[256,16,128]{2,1,0:T(8,128)(2,1)S(1)} %shard_map.64) | data formatting | bytes 2097152
Async XLA Ops:
  0.7 0.7 %copy-start.3 = (s32[256]{0:T(256)S(1)}, s32[256]{0:T(256)}, u32[]{:S(2)}) copy-start(s32[256]{0:T(256)} %param.9) | copy-start | bytes 3076
  0.7 0.7 %copy-start.4 = (s32[1,18]{1,0:T(1,128)S(1)}, s32[1,18]{1,0:T(1,128)}, u32[]{:S(2)}) copy-start(s32[1,18]{1,0:T(1,128)} %list_ref.1) | copy-start | bytes 220
  1.3 1.2 %copy-start = (bf16[256,16,128]{2,1,0:T(8,128)(2,1)S(1)}, bf16[256,16,128]{2,1,0:T(8,128)(2,1)}, u32[]{:S(2)}) copy-start(bf16[256,16,128]{2,1,0:T(8,128)(2,1)} %q_ref.1) | copy-start | bytes 3145732
  2.6 0.9 %copy-start.1 = (bf16[128,8,128]{2,1,0:T(8,128)(2,1)S(1)}, bf16[128,8,128]{2,1,0:T(8,128)(2,1)}, u32[]{:S(2)}) copy-start(bf16[128,8,128]{2,1,0:T(8,128)(2,1)} %k_ref.1) | copy-start | bytes 786436
  3.5 0.9 %copy-start.2 = (bf16[128,8,128]{2,1,0:T(8,128)(2,1)S(1)}, bf16[128,8,128]{2,1,0:T(8,128)(2,1)}, u32[]{:S(2)}) copy-start(bf16[128,8,128]{2,1,0:T(8,128)(2,1)} %v_ref.1) | copy-start | bytes 786436
